TPU v7x, 256 devices: a 8x8x2 block of a 8x8x16 slice. The times are simulated.
256 devices in a mesh: clips: 2 (over z), tile: 16 (over y, core), tm: 8 (over x).
Axes of the slice: x: 8, y: 8, z: 2, core: 2. Of those that a mesh axis runs over, the one named last changes fastest.
The devices are a block of a 8x8x16 slice.
Arguments:
- clip_frames: bfloat16 [32, 64, 128, 256], P(('clips', 'tm'), 'tile'), parts along dimension 0, may hold values from -6 to 6
- weight_first: bfloat16 [3, 3, 3, 256, 256], replicated, may hold values from -0.078125 to 0.078125
- bias_first: float32 [256], replicated, may hold values from -3 to 3
- weight_second: bfloat16 [3, 3, 3, 256, 256], replicated, may hold values from -0.078125 to 0.078125
- bias_second: float32 [256], replicated, may hold values from -3 to 3
Outputs:
- pooled_frames: bfloat16 [16, 64, 128, 256], P(('clips', 'tm'), 'tile'), parts along dimension 0
There are 2 independent parts, one for each index of `clips`. A program takes and returns all parts, laid end to end along the dimension named above; an argument that names none is the same for every part. Nothing has to cross between parts.
All inputs are finite; a program needn't handle non-finite values.
Results may differ from a plain program's by a relative error of at most 0.0029.
Values may be sent and summed in bfloat16 or wider, within the bound.
A program may use at most 128 MiB of HBM per device.

v0:
```python
import jax
import jax.numpy as jnp
from jax import lax
from jax.sharding import PartitionSpec as P


def shifted(value, axis, steps):
    count = lax.axis_size(axis)
    first, last = (max(0, -steps), min(count, count - steps))
    return lax.ppermute(value, axis, [(source, source + steps) for source in range(first, last)])


def extended(x, sides, width):
    for axis, dim in sides:
        count, length = (lax.axis_size(axis), x.shape[dim])
        up = [(i, (i + 1) % count) for i in range(count - 1)]
        down = [(j, i) for i, j in up]
        last = lax.slice_in_dim(x, length - width, length, axis=dim)
        first = lax.slice_in_dim(x, 0, width, axis=dim)
        before = lax.ppermute(last, axis, up)
        after = lax.ppermute(first, axis, down)
        x = jnp.concatenate([before, x, after], axis=dim)
    return x


def causal_taps(padded_input, weight, bias):
    frame_count = padded_input.shape[0] - 2
    row_count = padded_input.shape[1] - 2
    width_cells = padded_input.shape[2]
    channels = padded_input.shape[3]
    widened = jnp.pad(padded_input, ((0, 0), (0, 0), (1, 1), (0, 0)))
    accumulated = jnp.zeros((frame_count, row_count, width_cells, channels), jnp.float32) + bias
    for depth_tap in range(3):
        for row_tap in range(3):
            slab_taps = jnp.concatenate(
                [
                    widened[
                        depth_tap : depth_tap + frame_count,
                        row_tap : row_tap + row_count,
                        width_tap : width_tap + width_cells,
                    ]
                    for width_tap in range(3)
                ],
                axis=-1,
            )
            product = jnp.dot(
                slab_taps.reshape(-1, 3 * channels),
                weight[depth_tap, row_tap].reshape(3 * channels, channels),
                preferred_element_type=jnp.float32,
            )
            accumulated = accumulated + product.reshape(
                frame_count, row_count, width_cells, channels
            )
    return accumulated


def context(tensor):
    before = shifted(tensor, "tm", 1)
    framed = jnp.concatenate([before, tensor], axis=0)
    return extended(framed, (("tile", 1),), 1)


def shards(clip_frames, weight_first, bias_first, weight_second, bias_second):
    hidden = jax.nn.silu(causal_taps(context(clip_frames), weight_first, bias_first)).astype(
        jnp.bfloat16
    )
    summed = clip_frames.astype(jnp.float32) + causal_taps(
        context(hidden), weight_second, bias_second
    )
    return ((summed[0::2] + summed[1::2]) * 0.5).astype(jnp.bfloat16)


def solution(mesh):
    in_specs = (P(("clips", "tm"), "tile", None, None), P(), P(), P(), P())
    out_specs = P(("clips", "tm"), "tile", None, None)
    return jax.shard_map(shards, mesh=mesh, in_specs=in_specs, out_specs=out_specs, check_vma=False)
```

profile of v0, /device:TPU:697, one launch (start us, length us, event | category | flops | bytes accessed | tf_op | source)
XLA Modules:
  0.0 83.6 jit_solution(4362438822098181193)
XLA Ops:
  0.0 2.4 %collective-permute-start = (bf16[2,4,128,256]{3,2,1,0:T(8,128)(2,1)}, bf16[2,4,128,256]{3,2,1,0:T(8,128)(2,1)S(1)}, u32[]{:S(2)}, u32[]{:S(2)}) collective-permute-start(bf16[2,4,128,256]{3,2,1,0:T(8,128)(2,1)} %param.5), channel_id=1, source_target_pairs={{0,1},{1,2},{2,3},{3,4},{4,5},{5,6},{6,7},{8,9},{9,10},{10,11},{11... | collective-permute-start | bytes 1572872 | tf_op jit(solution)/shard_map/ppermute | solution.py:10
  2.4 13.8 %collective-permute-done = bf16[2,4,128,256]{3,2,1,0:T(8,128)(2,1)S(1)} collective-permute-done((bf16[2,4,128,256]{3,2,1,0:T(8,128)(2,1)}, bf16[2,4,128,256]{3,2,1,0:T(8,128)(2,1)S(1)}, u32[]{:S(2)}, u32[]{:S(2)}) %collective-permute-start) | collective-permute-done | bytes 524320 | tf_op jit(solution)/shard_map/ppermute | solution.py:10
  16.2 1.1 %constant_dynamic-update-slice_fusion = bf16[4,4,128,256]{3,2,1,0:T(8,128)(2,1)S(1)} fusion(bf16[4,4,128,256]{3,2,1,0:T(8,128)(2,1)S(1)} %constant_dynamic-update-slice_fusion.1, bf16[2,4,128,256]{3,2,1,0:T(8,128)(2,1)} %param.5), kind=kLoop, calls=%fused_computation.163 | loop fusion | bytes 1048576 | tf_op jit(solution)/shard_map/concatenate | solution.py:59
  17.4 7.0 %collective-permute-start.1 = (bf16[4,1,128,256]{3,2,1,0:T(8,128)(2,1)S(1)}, bf16[4,1,128,256]{3,2,1,0:T(8,128)(2,1)S(1)}, u32[]{:S(2)}, u32[]{:S(2)}) collective-permute-start(bf16[4,1,128,256]{3,2,1,0:T(8,128)(2,1)S(1)} %get-tuple-element.76), channel_id=1, source_target_pairs={{0,8},{8,16},{16,24},{24,32},{32,40},{40,48},{48,56},{56,64},{64,7... | collective-permute-start | bytes 786440 | tf_op jit(solution)/shard_map/ppermute | solution.py:20
  24.4 2.0 %collective-permute-start.2 = (bf16[4,1,128,256]{3,2,1,0:T(8,128)(2,1)S(1)}, bf16[4,1,128,256]{3,2,1,0:T(8,128)(2,1)S(1)}, u32[]{:S(2)}, u32[]{:S(2)}) collective-permute-start(bf16[4,1,128,256]{3,2,1,0:T(8,128)(2,1)S(1)} %get-tuple-element.77), channel_id=1, source_target_pairs={{8,0},{16,8},{24,16},{32,24},{40,32},{48,40},{56,48},{64,56},{72,6... | collective-permute-start | bytes 786440 | tf_op jit(solution)/shard_map/ppermute | solution.py:21
  26.3 2.2 %fusion.204 = (bf16[1,1,3,256,256]{4,3,2,1,0:T(8,128)(2,1)S(1)}, bf16[1,1,3,256,256]{4,3,2,1,0:T(8,128)(2,1)S(1)}, bf16[1,1,3,256,256]{4,3,2,1,0:T(8,128)(2,1)S(...) fusion(bf16[3,3,3,256,256]{4,3,2,1,0:T(8,128)(2,1)} %param.6), kind=kLoop, calls=%fused_computation.184 | loop fusion | bytes 7077888 | tf_op jit(solution)/shard_map/slice | solution.py:48
  28.5 4.8 %collective-permute-done.2 = bf16[4,1,128,256]{3,2,1,0:T(8,128)(2,1)S(1)} collective-permute-done((bf16[4,1,128,256]{3,2,1,0:T(8,128)(2,1)S(1)}, bf16[4,1,128,256]{3,2,1,0:T(8,128)(2,1)S(1)}, u32[]{:S(2)}, u32[]{:S(2)}) %collective-permute-start.2) | collective-permute-done | bytes 262176 | tf_op jit(solution)/shard_map/ppermute | solution.py:21
  33.3 0.9 %fusion.7 = bf16[4,6,130,256]{3,2,1,0:T(8,128)(2,1)S(1)} fusion(bf16[4,1,128,256]{3,2,1,0:T(8,128)(2,1)S(1)} %collective-permute-done.2, bf16[4,4,128,256]{3,2,1,0:T(8,128)(2,1)S(1)} %constant_dynamic-update-slice_fusion, bf16[4,1,128,256]{3,2,1,0:T(8,128)(2,1)S(1)} %collective-permute-done.1), kind=kLoop, calls=%fused_computation.15 | loop fusion | flops 9584640 | bytes 3170304 | tf_op jit(solution)/shard_map/concatenate | solution.py:22
  34.2 3.2 %fusion.206 = (bf16[2,4,128,256]{3,2,1,0:T(8,128)(2,1)S(1)}, bf16[2,4,128,256]{3,2,1,0:T(8,128)(2,1)S(1)}, bf16[2,4,128,256]{3,2,1,0:T(8,128)(2,1)S(1)}, bf16[2,...) fusion(bf16[4,6,130,256]{3,2,1,0:T(8,128)(2,1)S(1)} %fusion.7), kind=kLoop, calls=%fused_computation.186 | loop fusion | bytes 18874368 | tf_op jit(solution)/shard_map/slice | solution.py:37
  38.2 0.6 fusion.36
  38.8 0.6 fusion.42
  39.4 0.6 fusion.48
  42.5 0.9 %multiply_convert_fusion = bf16[2,4,128,256]{3,2,1,0:T(8,128)(2,1)S(1)} fusion(f32[2,4,128,256]{3,2,1,0:T(8,128)S(1)} %fusion.16, f32[2,4,128,256]{3,2,1,0:T(8,128)S(1)} %fusion.62, f32[2,4,128,256]{3,2,1,0:T(8,128)S(1)} %fusion.21, f32[2,4,128,256]{3,2,1,0:T(8,128)S(1)} %fusion.54, f32[2,4,128,256]{3,2,1,0:T(8,128)S(1)} %fusion.48, ...), kind=kOutput, calls=%fused_computation.153 | convolution fusion | flops 411041792 | bytes 10880000 | tf_op jit(solution)/shard_map/dot_general | solution.py:46
  43.4 2.1 %collective-permute-start.3 = (bf16[2,4,128,256]{3,2,1,0:T(8,128)(2,1)S(1)}, bf16[2,4,128,256]{3,2,1,0:T(8,128)(2,1)S(1)}, u32[]{:S(2)}, u32[]{:S(2)}) collective-permute-start(bf16[2,4,128,256]{3,2,1,0:T(8,128)(2,1)S(1)} %multiply_convert_fusion), channel_id=1, source_target_pairs={{0,1},{1,2},{2,3},{3,4},{4,5},{5,6},{6,7},{8,9},{9,10},{10,11},{11... | collective-permute-start | bytes 1572872 | tf_op jit(solution)/shard_map/ppermute | solution.py:10
  45.5 10.3 %collective-permute-done.3 = bf16[2,4,128,256]{3,2,1,0:T(8,128)(2,1)S(1)} collective-permute-done((bf16[2,4,128,256]{3,2,1,0:T(8,128)(2,1)S(1)}, bf16[2,4,128,256]{3,2,1,0:T(8,128)(2,1)S(1)}, u32[]{:S(2)}, u32[]{:S(2)}) %collective-permute-start.3) | collective-permute-done | bytes 524320 | tf_op jit(solution)/shard_map/ppermute | solution.py:10
  55.8 7.4 %collective-permute-start.4 = (bf16[4,1,128,256]{3,2,1,0:T(8,128)(2,1)S(1)}, bf16[4,1,128,256]{3,2,1,0:T(8,128)(2,1)S(1)}, u32[]{:S(2)}, u32[]{:S(2)}) collective-permute-start(bf16[4,1,128,256]{3,2,1,0:T(8,128)(2,1)S(1)} %get-tuple-element.71), channel_id=1, source_target_pairs={{0,8},{8,16},{16,24},{24,32},{32,40},{40,48},{48,56},{56,64},{64,7... | collective-permute-start | bytes 786440 | tf_op jit(solution)/shard_map/ppermute | solution.py:20
  63.3 2.1 %collective-permute-start.5 = (bf16[4,1,128,256]{3,2,1,0:T(8,128)(2,1)S(1)}, bf16[4,1,128,256]{3,2,1,0:T(8,128)(2,1)S(1)}, u32[]{:S(2)}, u32[]{:S(2)}) collective-permute-start(bf16[4,1,128,256]{3,2,1,0:T(8,128)(2,1)S(1)} %get-tuple-element.72), channel_id=1, source_target_pairs={{8,0},{16,8},{24,16},{32,24},{40,32},{48,40},{56,48},{64,56},{72,6... | collective-permute-start | bytes 786440 | tf_op jit(solution)/shard_map/ppermute | solution.py:21
  65.7 0.9 %collective-permute-done.4 = bf16[4,1,128,256]{3,2,1,0:T(8,128)(2,1)S(1)} collective-permute-done((bf16[4,1,128,256]{3,2,1,0:T(8,128)(2,1)S(1)}, bf16[4,1,128,256]{3,2,1,0:T(8,128)(2,1)S(1)}, u32[]{:S(2)}, u32[]{:S(2)}) %collective-permute-start.4) | collective-permute-done | bytes 262176 | tf_op jit(solution)/shard_map/ppermute | solution.py:20
  66.6 5.6 %collective-permute-done.5 = bf16[4,1,128,256]{3,2,1,0:T(8,128)(2,1)S(1)} collective-permute-done((bf16[4,1,128,256]{3,2,1,0:T(8,128)(2,1)S(1)}, bf16[4,1,128,256]{3,2,1,0:T(8,128)(2,1)S(1)}, u32[]{:S(2)}, u32[]{:S(2)}) %collective-permute-start.5) | collective-permute-done | bytes 262176 | tf_op jit(solution)/shard_map/ppermute | solution.py:21
  72.2 1.0 %select_maximum_fusion = bf16[4,6,130,256]{3,2,1,0:T(8,128)(2,1)S(1)} fusion(bf16[4,1,128,256]{3,2,1,0:T(8,128)(2,1)S(1)} %collective-permute-done.5, bf16[4,1,128,256]{3,2,1,0:T(8,128)(2,1)S(1)} %collective-permute-done.4, bf16[2,4,128,256]{3,2,1,0:T(8,128)(2,1)S(1)} %multiply_convert_fusion, bf16[2,4,128,256]{3,2,1,0:T(8,128)(2,1)S(1)} %collective-permute-done.3), kind=kLoop, calls=%fused_computation.7 | loop fusion | flops 11980800 | bytes 3170304 | tf_op jit(solution)/shard_map/concatenate | solution.py:22
  73.2 3.2 %fusion.205 = (bf16[2,4,128,256]{3,2,1,0:T(8,128)(2,1)S(1)}, bf16[2,4,128,256]{3,2,1,0:T(8,128)(2,1)S(1)}, bf16[2,4,128,256]{3,2,1,0:T(8,128)(2,1)S(1)}, bf16[2,...) fusion(bf16[4,6,130,256]{3,2,1,0:T(8,128)(2,1)S(1)} %select_max, ...), kind=kLoop, calls=%fused_computation.185 | loop fusion | bytes 18874368 | tf_op jit(solution)/shard_map/slice | solution.py:37
  77.0 0.6 fusion.108
  81.8 1.0 %fusion.156 = f32[2,4,128,256]{3,2,1,0:T(8,128)S(1)} fusion(f32[2,4,128,256]{3,2,1,0:T(8,128)S(1)} %fusion.114, f32[2,4,128,256]{3,2,1,0:T(8,128)S(1)} %fusion.108, f32[2,4,128,256]{3,2,1,0:T(8,128)S(1)} %fusion.102, f32[2,4,128,256]{3,2,1,0:T(8,128)S(1)} %fusion.96, f32[2,4,128,256]{3,2,1,0:T(8,128)S(1)} %fusion.11, f32[2,4,128,256]{3,2,1,0:T(8,128)S(1)} %fusion.88, ...), kind=kOutput, calls=%fused_computation.140 | convolution fusion | flops 410255360 | bytes 11928576 | tf_op jit(solution)/shard_map/dot_general | solution.py:46
  82.8 0.8 fusion.184
  (28 shorter events, 8.2 us)
Async XLA Ops:
  0.0 16.2 %collective-permute-start = (bf16[2,4,128,256]{3,2,1,0:T(8,128)(2,1)}, bf16[2,4,128,256]{3,2,1,0:T(8,128)(2,1)S(1)}, u32[]{:S(2)}, u32[]{:S(2)}) collective-permute-start(bf16[2,4,128,256]{3,2,1,0:T(8,128)(2,1)} %param.5), channel_id=1, source_target_pairs={{0,1},{1,2},{2,3},{3,4},{4,5},{5,6},{6,7},{8,9},{9,10},{10,11},{11... | collective-permute-start | bytes 1572872 | tf_op jit(solution)/shard_map/ppermute | solution.py:10
  17.4 11.2 %collective-permute-start.1 = (bf16[4,1,128,256]{3,2,1,0:T(8,128)(2,1)S(1)}, bf16[4,1,128,256]{3,2,1,0:T(8,128)(2,1)S(1)}, u32[]{:S(2)}, u32[]{:S(2)}) collective-permute-start(bf16[4,1,128,256]{3,2,1,0:T(8,128)(2,1)S(1)} %get-tuple-element.76), channel_id=1, source_target_pairs={{0,8},{8,16},{16,24},{24,32},{32,40},{40,48},{48,56},{56,64},{64,7... | collective-permute-start | bytes 786440 | tf_op jit(solution)/shard_map/ppermute | solution.py:20
  24.4 8.9 %collective-permute-start.2 = (bf16[4,1,128,256]{3,2,1,0:T(8,128)(2,1)S(1)}, bf16[4,1,128,256]{3,2,1,0:T(8,128)(2,1)S(1)}, u32[]{:S(2)}, u32[]{:S(2)}) collective-permute-start(bf16[4,1,128,256]{3,2,1,0:T(8,128)(2,1)S(1)} %get-tuple-element.77), channel_id=1, source_target_pairs={{8,0},{16,8},{24,16},{32,24},{40,32},{48,40},{56,48},{64,56},{72,6... | collective-permute-start | bytes 786440 | tf_op jit(solution)/shard_map/ppermute | solution.py:21
  34.2 3.3 %copy-start.1 = (bf16[2,4,128,256]{3,2,1,0:T(8,128)(2,1)S(1)}, bf16[2,4,128,256]{3,2,1,0:T(8,128)(2,1)}, u32[]{:S(2)}) copy-start(bf16[2,4,128,256]{3,2,1,0:T(8,128)(2,1)} %param.5) | copy-start | bytes 1572868
  41.8 0.7 copy-start.3
  42.5 23.0 %copy-start = (bf16[3,3,3,256,256]{4,3,2,1,0:T(8,128)(2,1)S(1)}, bf16[3,3,3,256,256]{4,3,2,1,0:T(8,128)(2,1)}, u32[]{:S(2)}) copy-start(bf16[3,3,3,256,256]{4,3,2,1,0:T(8,128)(2,1)} %param.8) | copy-start | bytes 10616836
  43.4 12.4 %collective-permute-start.3 = (bf16[2,4,128,256]{3,2,1,0:T(8,128)(2,1)S(1)}, bf16[2,4,128,256]{3,2,1,0:T(8,128)(2,1)S(1)}, u32[]{:S(2)}, u32[]{:S(2)}) collective-permute-start(bf16[2,4,128,256]{3,2,1,0:T(8,128)(2,1)S(1)} %multiply_convert_fusion), channel_id=1, source_target_pairs={{0,1},{1,2},{2,3},{3,4},{4,5},{5,6},{6,7},{8,9},{9,10},{10,11},{11... | collective-permute-start | bytes 1572872 | tf_op jit(solution)/shard_map/ppermute | solution.py:10
  55.8 10.7 %collective-permute-start.4 = (bf16[4,1,128,256]{3,2,1,0:T(8,128)(2,1)S(1)}, bf16[4,1,128,256]{3,2,1,0:T(8,128)(2,1)S(1)}, u32[]{:S(2)}, u32[]{:S(2)}) collective-permute-start(bf16[4,1,128,256]{3,2,1,0:T(8,128)(2,1)S(1)} %get-tuple-element.71), channel_id=1, source_target_pairs={{0,8},{8,16},{16,24},{24,32},{32,40},{40,48},{48,56},{56,64},{64,7... | collective-permute-start | bytes 786440 | tf_op jit(solution)/shard_map/ppermute | solution.py:20
  63.3 8.9 %collective-permute-start.5 = (bf16[4,1,128,256]{3,2,1,0:T(8,128)(2,1)S(1)}, bf16[4,1,128,256]{3,2,1,0:T(8,128)(2,1)S(1)}, u32[]{:S(2)}, u32[]{:S(2)}) collective-permute-start(bf16[4,1,128,256]{3,2,1,0:T(8,128)(2,1)S(1)} %get-tuple-element.72), channel_id=1, source_target_pairs={{8,0},{16,8},{24,16},{32,24},{40,32},{48,40},{56,48},{64,56},{72,6... | collective-permute-start | bytes 786440 | tf_op jit(solution)/shard_map/ppermute | solution.py:21
  81.1 0.7 copy-start.2
where the time goes:
time: 83.9 us; the launch traced here: 83.6 us
  waiting for transfers between devices  35.4 us (42%)
  starting transfers between devices  23 us (27%)
  matrix products  11.2 us (13%)
  local copies, waits for them, and re-layouts  10.6 us (13%)
  other arithmetic  3.06 us (4%)
    ppermute x2, waiting for transfers between devices, shifted(): lax.ppermute(value, axis, [(source, source + steps) for source in range(f...  24.1 us
    ppermute x2, starting transfers between devices, extended(): before = lax.ppermute(last, axis, up)  14.4 us
    dot_general x18, matrix products, causal_taps(): jnp.dot(slab_taps.reshape(-1, 3 * channels), weight[depth_tap, row_tap].r...  11.2 us
    ppermute x2, waiting for transfers between devices, extended(): after = lax.ppermute(first, axis, down)  10.4 us
    slice x3, local copies, waits for them, and re-layouts, causal_taps(): widened[depth_tap:depth_tap + frame_count, row_tap:row_tap + row_count, w...  6.83 us
    ppermute x2, starting transfers between devices, shifted(): lax.ppermute(value, axis, [(source, source + steps) for source in range(f...  4.46 us
    ppermute x2, starting transfers between devices, extended(): after = lax.ppermute(first, axis, down)  4.08 us
    slice x2, local copies, waits for them, and re-layouts, causal_taps(): weight[depth_tap, row_tap].reshape(3 * channels, channels)  2.42 us
  transfers between devices with their start and end apart: 6, of which 5 were waited for; matrix products, arithmetic and copies ran while one was open for 3% of the time, Pallas kernels for 0%

commit v1 on v0

v1 whole, which is shorter than its diff:
```python
import jax
import jax.numpy as jnp
from jax import lax
from jax.experimental import pallas as pl
from jax.experimental.pallas import tpu as pltpu
from jax.sharding import PartitionSpec as P

MESH = pl.DeviceIdType.MESH
PAD = 8
F32 = jnp.float32
BF16 = jnp.bfloat16


def mm(a, b):
    return jnp.dot(a, b, preferred_element_type=F32)


def bounds(width):
    step = width // 4
    xs = [0, step + 16, 2 * step + 16, 3 * step + 16, width]
    hs = [0, step, 2 * step, 3 * step, width]
    os = [0, step - 16, 2 * step - 16, 3 * step - 16, width]
    return xs, hs, os


def kernel(
    x_hbm, w1_hbm, b1_ref, w2_hbm, b2_ref, out_hbm,
    xo, xh, w1, w2, w01, acc, hs, oq, nq, ob, ns, nr, outv,
    ld, st, xs_s, xs_r, ro_s, ro_r, fw_s, fw_r, he_s, he_r, n_s, n_r,
):
    frames, rows, width, chans = x_hbm.shape
    xb, hb, pb = bounds(width)
    chunks = len(xb) - 1
    i, j = lax.axis_index("tm"), lax.axis_index("tile")
    ni, nj = lax.axis_size("tm"), lax.axis_size("tile")
    has_prev, has_next = i > 0, i < ni - 1
    has_up, has_dn = j > 0, j < nj - 1
    prev, nxt = {"tm": i - 1}, {"tm": i + 1}
    up, dn = {"tile": j - 1}, {"tile": j + 1}
    last = rows

    def local(src, dst, sem):
        return pltpu.make_async_copy(src, dst, sem)

    def remote(src, dst, ssem, rsem, dev):
        return pltpu.make_async_remote_copy(
            src_ref=src, dst_ref=dst, send_sem=ssem, recv_sem=rsem, device_id=dev, device_id_type=MESH
        )

    load_x = local(x_hbm, xo.at[:, 1 : rows + 1], ld.at[0])
    load_w1 = local(w1_hbm, w1, ld.at[1])
    load_w2 = local(w2_hbm, w2, ld.at[2])
    load_x.start()
    load_w1.start()
    load_w2.start()

    barrier = pltpu.get_barrier_semaphore()
    for cond, dev in ((has_prev, prev), (has_up, up), (has_dn, dn)):
        @pl.when(cond)
        def _(dev=dev):
            pl.semaphore_signal(barrier, inc=1, device_id=dev, device_id_type=MESH)

    for buf in (oq, nq):
        for q, at in ((0, 0), (2, PAD + width)):
            buf[q, :, at : at + PAD, :] = jnp.zeros((rows, PAD, chans), F32)
    for q, at in ((0, 0), (2, PAD + width)):
        acc[q, :, :, at : at + PAD, :] = jnp.zeros((frames, rows, PAD, chans), F32)

    @pl.when(jnp.logical_not(has_prev))
    def _():
        xh[...] = jnp.zeros(xh.shape, BF16)
        nr[...] = jnp.zeros(nr.shape, BF16)

    for cond, row in ((has_up, 0), (has_dn, last + 1)):
        @pl.when(jnp.logical_not(cond))
        def _(row=row):
            zero = jnp.zeros((frames, width, chans), BF16)
            xo[:, row] = zero
            xh[:, row] = zero
            hs[:, row] = zero

    load_x.wait()
    pl.semaphore_wait(barrier, sum(cond.astype(jnp.int32) for cond in (has_next, has_up, has_dn)))

    def rowcopy(buf, c0, c1, s, r, k, down):
        if down:
            return remote(buf.at[:, last, c0:c1], buf.at[:, 0, c0:c1], s.at[k], r.at[k], dn)
        return remote(buf.at[:, 1, c0:c1], buf.at[:, last + 1, c0:c1], s.at[k], r.at[k], up)

    own_up = rowcopy(xo, 0, width, ro_s, ro_r, 0, False)
    own_dn = rowcopy(xo, 0, width, ro_s, ro_r, 1, True)
    edges, middle = [], []
    for c in range(chunks):
        c0, c1 = xb[c], xb[c + 1]
        edges.append([
            remote(xo.at[:, row, c0:c1], xh.at[:, row, c0:c1], xs_s.at[3 * c + k], xs_r.at[3 * c + k], nxt)
            for k, row in enumerate((1, last))
        ])
        middle.append(
            remote(xo.at[:, 2:last, c0:c1], xh.at[:, 2:last, c0:c1], xs_s.at[3 * c + 2], xs_r.at[3 * c + 2], nxt)
        )
    fwd = [
        (rowcopy(xh, xb[c], xb[c + 1], fw_s, fw_r, 2 * c, False),
         rowcopy(xh, xb[c], xb[c + 1], fw_s, fw_r, 2 * c + 1, True))
        for c in range(chunks)
    ]
    hid = [
        (rowcopy(hs, hb[c], hb[c + 1], he_s, he_r, 2 * c, False),
         rowcopy(hs, hb[c], hb[c + 1], he_s, he_r, 2 * c + 1, True))
        for c in range(chunks)
    ]
    part = [
        remote(ns.at[:, pb[c] : pb[c + 1]], nr.at[:, pb[c] : pb[c + 1]], n_s.at[c], n_r.at[c], nxt)
        for c in range(chunks)
    ]

    @pl.when(has_next)
    def _():
        for pair in edges:
            for copy in pair:
                copy.start()
        for copy in middle:
            copy.start()

    @pl.when(has_up)
    def _():
        own_up.start()

    @pl.when(has_dn)
    def _():
        own_dn.start()

    load_w2.wait()
    w01[...] = (w2[0].astype(F32) + w2[1].astype(F32)).astype(BF16)
    load_w1.wait()

    @pl.when(has_dn)
    def _():
        own_up.wait_recv()

    @pl.when(has_up)
    def _():
        own_dn.wait_recv()

    def forward(c):
        @pl.when(has_prev)
        def _():
            for copy in edges[c]:
                copy.wait_recv()

        @pl.when(has_prev & has_up)
        def _():
            fwd[c][0].start()

        @pl.when(has_prev & has_dn)
        def _():
            fwd[c][1].start()

    def own_tap(q):
        both = first = None
        for p in range(3):
            v = xo[:, p : p + rows].reshape(frames * rows * width, chans)
            a = mm(v, w1[2, p, q])
            b = mm(v[: rows * width], w1[1, p, q])
            both = a if both is None else both + a
            first = b if first is None else first + b
        inside = slice(PAD, PAD + width)
        acc[q, 0, :, inside, :] = both[: rows * width].reshape(rows, width, chans)
        acc[q, 1, :, inside, :] = (both[rows * width :] + first).reshape(rows, width, chans)

    for c in range(chunks):
        forward(c)
        if c < 3:
            own_tap(c)

    def shifted_sum(ref, c0, c1):
        return sum(ref[q, ..., PAD - 1 + q + c0 : PAD - 1 + q + c1, :] for q in range(3))

    bias1 = b1_ref[...].reshape(1, 1, chans)
    bias2 = b2_ref[...].reshape(1, 1, chans)

    def first_conv(c):
        @pl.when(has_prev)
        def _():
            middle[c].wait_recv()

        @pl.when(has_prev & has_dn)
        def _():
            fwd[c][0].wait_recv()

        @pl.when(has_prev & has_up)
        def _():
            fwd[c][1].wait_recv()

        c0, c1 = xb[c], xb[c + 1]
        size = rows * (c1 - c0)
        for q in range(3):
            both = second = None
            for p in range(3):
                v = xh[:, p : p + rows, c0:c1].reshape(frames * size, chans)
                a = mm(v, w1[0, p, q])
                b = mm(v[size:], w1[1, p, q])
                both = a if both is None else both + a
                second = b if second is None else second + b
            inside = slice(PAD + c0, PAD + c1)
            acc[q, 0, :, inside, :] += (both[:size] + second).reshape(rows, c1 - c0, chans)
            acc[q, 1, :, inside, :] += both[size:].reshape(rows, c1 - c0, chans)
        h0, h1 = hb[c], hb[c + 1]
        y = [shifted_sum(acc.at[:, f], h0, h1) + bias1 for f in range(2)]
        y = [(v / (1.0 + jnp.exp(-v))).astype(BF16) for v in y]
        hs[0, 1 : rows + 1, h0:h1] = y[0]
        hs[1, 1 : rows + 1, h0:h1] = (y[0].astype(F32) + y[1].astype(F32)).astype(BF16)

        @pl.when(has_up)
        def _():
            hid[c][0].start()

        @pl.when(has_dn)
        def _():
            hid[c][1].start()

    def second_conv(c):
        @pl.when(has_dn)
        def _():
            hid[c][0].wait_recv()

        @pl.when(has_up)
        def _():
            hid[c][1].wait_recv()

        h0, h1 = hb[c], hb[c + 1]
        size = rows * (h1 - h0)
        for q in range(3):
            one = two = mix = None
            for p in range(3):
                v = hs[0, p : p + rows, h0:h1].reshape(size, chans)
                u = hs[1, p : p + rows, h0:h1].reshape(size, chans)
                a, b, d = mm(v, w2[1, p, q]), mm(u, w2[2, p, q]), mm(u, w01[p, q])
                one = a if one is None else one + a
                two = b if two is None else two + b
                mix = d if mix is None else mix + d
            inside = slice(PAD + h0, PAD + h1)
            oq[q, :, inside, :] = (one + two).reshape(rows, h1 - h0, chans)
            nq[q, :, inside, :] = (mix - one).reshape(rows, h1 - h0, chans)
        p0, p1 = pb[c], pb[c + 1]
        ns[:, p0:p1] = shifted_sum(nq, p0, p1).astype(BF16)

        @pl.when(has_next)
        def _():
            part[c].start()

        own = xo[0, 1 : rows + 1, p0:p1].astype(F32) + xo[1, 1 : rows + 1, p0:p1].astype(F32)
        ob[:, p0:p1] = 0.5 * (shifted_sum(oq, p0, p1) + own) + bias2

    first_conv(0)
    for c in range(1, chunks):
        first_conv(c)
        second_conv(c - 1)
    second_conv(chunks - 1)

    stores = []
    for c in range(chunks):
        @pl.when(has_prev)
        def _():
            part[c].wait_recv()

        p0, p1 = pb[c], pb[c + 1]
        outv[:, p0:p1] = (ob[:, p0:p1] + 0.5 * nr[:, p0:p1].astype(F32)).astype(BF16)
        store = local(outv.at[:, p0:p1], out_hbm.at[0, :, p0:p1], st.at[c])
        store.start()
        stores.append(store)

    @pl.when(has_next)
    def _():
        for c in range(chunks):
            for copy in (*edges[c], middle[c], part[c]):
                copy.wait_send()

    @pl.when(has_up)
    def _():
        own_up.wait_send()
        for c in range(chunks):
            hid[c][0].wait_send()

    @pl.when(has_dn)
    def _():
        own_dn.wait_send()
        for c in range(chunks):
            hid[c][1].wait_send()

    @pl.when(has_prev & has_up)
    def _():
        for c in range(chunks):
            fwd[c][0].wait_send()

    @pl.when(has_prev & has_dn)
    def _():
        for c in range(chunks):
            fwd[c][1].wait_send()

    for store in stores:
        store.wait()


def shards(x, w1, b1, w2, b2):
    frames, rows, width, chans = x.shape
    chunks = len(bounds(width)[0]) - 1
    dma = pltpu.SemaphoreType.DMA
    hbm, vmem = pl.BlockSpec(memory_space=pltpu.HBM), pl.BlockSpec(memory_space=pltpu.VMEM)
    extended = pltpu.VMEM((frames, rows + 2, width, chans), BF16)
    taps = pltpu.VMEM((3, rows, width + 2 * PAD, chans), F32)
    flat = pltpu.VMEM((rows, width, chans), BF16)
    return pl.pallas_call(
        kernel,
        out_shape=jax.ShapeDtypeStruct((1, rows, width, chans), BF16),
        in_specs=[hbm, hbm, vmem, hbm, vmem],
        out_specs=hbm,
        scratch_shapes=[
            extended, extended,
            pltpu.VMEM(w1.shape, BF16), pltpu.VMEM(w2.shape, BF16), pltpu.VMEM(w2.shape[1:], BF16),
            pltpu.VMEM((3, frames, rows, width + 2 * PAD, chans), F32),
            extended, taps, taps, pltpu.VMEM((rows, width, chans), F32),
            flat, flat, flat,
            dma((3,)), dma((chunks,)),
            dma((3 * chunks,)), dma((3 * chunks,)),
            dma((2,)), dma((2,)),
            dma((2 * chunks,)), dma((2 * chunks,)),
            dma((2 * chunks,)), dma((2 * chunks,)),
            dma((chunks,)), dma((chunks,)),
        ],
        compiler_params=pltpu.CompilerParams(
            collective_id=0, has_side_effects=True, vmem_limit_bytes=67043328
        ),
    )(x, w1, b1.reshape(1, chans), w2, b2.reshape(1, chans))


def solution(mesh):
    spec = P(("clips", "tm"), "tile", None, None)
    return jax.shard_map(shards, mesh=mesh, in_specs=(spec, P(), P(), P(), P()), out_specs=spec, check_vma=False)
```

time: 83.9 us -> 45.7 us (0.54)
  the two profiles are of different devices: /device:TPU:697 before, /device:TPU:516 now
where the time goes in v1:
time: 45.7 us; the launch traced here: 45.6 us
  Pallas kernels  43.9 us (96%)
  local copies, waits for them, and re-layouts  1.67 us (4%)
    pallas_call x1, Pallas kernels, shards(): pl.pallas_call(kernel, out_shape=jax.ShapeDtypeStruct((1, rows, width, ch...  43.9 us
    unnamed x1, local copies, waits for them, and re-layouts  1.67 us

profile of v1, /device:TPU:516, one launch (start us, length us, event | category | flops | bytes accessed | tf_op | source)
XLA Modules:
  0.0 45.6 jit_solution(15468111767719596949)
XLA Ops:
  0.0 43.9 %shard_map.55 = bf16[1,4,128,256]{3,2,1,0:T(8,128)(2,1)} custom-call(bf16[2,4,128,256]{3,2,1,0:T(8,128)(2,1)} %x_hbm.1, bf16[3,3,3,256,256]{4,3,2,1,0:T(8,128)(2,1)} %w1_hbm.1, f32[1,256]{1,0:T(1,128)} %bitcast.2, bf16[3,3,3,256,256]{4,3,2,1,0:T(8,128)(2,1)} %w2_hbm.1, f32[1,256]{1,0:T(1,128)} %bitcast.3), custom_call_target="tpu_custom_call" | custom-call | tf_op jit(solution)/shard_map/pallas_call | solution.py:313
  43.9 1.7 %copy.7 = bf16[1,4,128,256]{3,2,1,0:T(8,128)(2,1)} copy(bf16[1,4,128,256]{3,2,1,0:T(8,128)(2,1)} %shard_map.55) | data formatting | bytes 524288

commit v2 on v1

--- a/solution.py
+++ b/solution.py
@@ -1,3 +1,5 @@
+import functools
+
 import jax
 import jax.numpy as jnp
 from jax import lax
@@ -11,8 +13,23 @@
 BF16 = jnp.bfloat16
 
 
-def mm(a, b):
-    return jnp.dot(a, b, preferred_element_type=F32)
+def matmuls(jobs):
+    units = range(len(jobs))
+    for m in units:
+        pltpu.matmul_push_rhs(jobs[m][0][0](), staging_register=0, mxu_index=m)
+    for k in range(max(len(job) for job in jobs)):
+        for m in units:
+            if k + 1 < len(jobs[m]):
+                pltpu.matmul_push_rhs(jobs[m][k + 1][0](), staging_register=(k + 1) % 2, mxu_index=m)
+        for m in units:
+            if k < len(jobs[m]):
+                for n, (acc, left) in enumerate(jobs[m][k][1]):
+                    pltpu.matmul_acc_lhs(acc, left(), load_staged_rhs=k % 2 if n == 0 else None)
+
+
+def accumulators(body, size, count):
+    spec = [pltpu.ACC(m)((size, 256), F32) for m in (0, 1) for _ in range(count)]
+    pl.run_scoped(lambda *accs: body(accs[:count], accs[count:]), *spec)
 
 
 def bounds(width):
@@ -24,9 +41,9 @@
 
 
 def kernel(
-    x_hbm, w1_hbm, b1_ref, w2_hbm, b2_ref, out_hbm,
-    xo, xh, w1, w2, w01, acc, hs, oq, nq, ob, ns, nr, outv,
-    ld, st, xs_s, xs_r, ro_s, ro_r, fw_s, fw_r, he_s, he_r, n_s, n_r,
+    x_hbm, w1_hbm, b1_ref, w2_hbm, b2_ref, out,
+    xo, xh, w1, w2, w01, acc, hs, oq, nq, ob, ns, nr,
+    ld, ready, xs_s, xs_r, ro_s, ro_r, fw_s, fw_r, he_s, he_r, n_s, n_r,
 ):
     frames, rows, width, chans = x_hbm.shape
     xb, hb, pb = bounds(width)
@@ -48,14 +65,18 @@
         )
 
     load_x = local(x_hbm, xo.at[:, 1 : rows + 1], ld.at[0])
-    load_w1 = local(w1_hbm, w1, ld.at[1])
-    load_w2 = local(w2_hbm, w2, ld.at[2])
+    load_w1_own = local(w1_hbm.at[1:3], w1.at[1:3], ld.at[1])
+    load_w1_prev = local(w1_hbm.at[0], w1.at[0], ld.at[2])
+    load_w2 = local(w2_hbm, w2, ld.at[3])
     load_x.start()
-    load_w1.start()
+    load_w1_own.start()
+    load_w1_prev.start()
     load_w2.start()
 
     barrier = pltpu.get_barrier_semaphore()
-    for cond, dev in ((has_prev, prev), (has_up, up), (has_dn, dn)):
+    odd = lax.rem(j, 2) == 1
+    even = jnp.logical_not(odd)
+    for cond, dev in ((has_prev, prev), (has_up & odd, up), (has_dn & odd, dn)):
         @pl.when(cond)
         def _(dev=dev):
             pl.semaphore_signal(barrier, inc=1, device_id=dev, device_id_type=MESH)
@@ -68,7 +89,6 @@
 
     @pl.when(jnp.logical_not(has_prev))
     def _():
-        xh[...] = jnp.zeros(xh.shape, BF16)
         nr[...] = jnp.zeros(nr.shape, BF16)
 
     for cond, row in ((has_up, 0), (has_dn, last + 1)):
@@ -79,8 +99,13 @@
             xh[:, row] = zero
             hs[:, row] = zero
 
+    accumulators(lambda unit0, unit1: [pltpu.matmul_pop(a) for a in (*unit0, *unit1)] and None, 1024, 1)
     load_x.wait()
-    pl.semaphore_wait(barrier, sum(cond.astype(jnp.int32) for cond in (has_next, has_up, has_dn)))
+    peers = sum(cond.astype(jnp.int32) for cond in (has_next, has_up & even, has_dn & even))
+
+    @pl.when(peers > 0)
+    def _():
+        pl.semaphore_wait(barrier, peers)
 
     def rowcopy(buf, c0, c1, s, r, k, down):
         if down:
@@ -122,56 +147,89 @@
         for copy in middle:
             copy.start()
 
+    @pl.when(has_up & even)
+    def _():
+        pl.semaphore_signal(ready.at[0], inc=1, device_id=up, device_id_type=MESH)
+        own_up.start()
+
+    @pl.when(has_dn & even)
+    def _():
+        pl.semaphore_signal(ready.at[1], inc=1, device_id=dn, device_id_type=MESH)
+        own_dn.start()
+
+    @pl.when(has_dn & odd)
+    def _():
+        pl.semaphore_wait(ready.at[0], 1)
+        own_dn.start()
+
+    @pl.when(has_up & odd)
+    def _():
+        pl.semaphore_wait(ready.at[1], 1)
+        own_up.start()
+
+    @pl.when(has_dn)
+    def _():
+        own_up.wait_recv()
+
     @pl.when(has_up)
     def _():
-        own_up.start()
-
-    @pl.when(has_dn)
-    def _():
-        own_dn.start()
-
+        own_dn.wait_recv()
+
+    def forward(c):
+        @pl.when(has_prev)
+        def _():
+            for copy in edges[c]:
+                copy.wait_recv()
+
+        @pl.when(has_prev & has_up)
+        def _():
+            fwd[c][0].start()
+
+        @pl.when(has_prev & has_dn)
+        def _():
+            fwd[c][1].start()
+
+    def own_half(r0, unit0, unit1):
+        def left(f, p):
+            return lambda: xo[f, r0 + p : r0 + p + 2].reshape(2 * width, chans)
+
+        def pair(accs, q, p):
+            return (lambda: w1[2, p, q]), [(accs[0], left(0, p)), (accs[1], left(1, p))]
+
+        def single(accs, q, p):
+            return (lambda: w1[1, p, q]), [(accs[1], left(0, p))]
+
+        jobs = first_jobs(unit0, unit1, pair, single)
+        matmuls(jobs)
+        store_taps(unit0, unit1, lambda v: v.reshape(2, width, chans), slice(r0, r0 + 2), slice(PAD, PAD + width), False)
+
+    def first_jobs(unit0, unit1, pair, single):
+        out = []
+        for accs, q, extra in ((unit0, 0, ((pair, 0), (single, 0), (single, 1))), (unit1, 2, ((pair, 1), (pair, 2), (single, 2)))):
+            job = []
+            for p in range(3):
+                job += [pair(accs[:2], q, p), single(accs[:2], q, p)]
+            out.append(job + [kind(accs[2:], 1, p) for kind, p in extra])
+        return out
+
+    def store_taps(unit0, unit1, shape, rws, cols, add):
+        for f in range(2):
+            parts = (unit0[f], unit0[2 + f], unit1[f], unit1[2 + f])
+            zero, one0, two, one1 = (shape(pltpu.matmul_pop(part)) for part in parts)
+            for q, value in ((0, zero), (1, one0 + one1), (2, two)):
+                if add:
+                    acc[q, f, rws, cols, :] += value
+                else:
+                    acc[q, f, rws, cols, :] = value
+
+    load_w1_own.wait()
+    for r0 in (0, 2):
+        accumulators(functools.partial(own_half, r0), 2 * width, 4)
     load_w2.wait()
     w01[...] = (w2[0].astype(F32) + w2[1].astype(F32)).astype(BF16)
-    load_w1.wait()
-
-    @pl.when(has_dn)
-    def _():
-        own_up.wait_recv()
-
-    @pl.when(has_up)
-    def _():
-        own_dn.wait_recv()
-
-    def forward(c):
-        @pl.when(has_prev)
-        def _():
-            for copy in edges[c]:
-                copy.wait_recv()
-
-        @pl.when(has_prev & has_up)
-        def _():
-            fwd[c][0].start()
-
-        @pl.when(has_prev & has_dn)
-        def _():
-            fwd[c][1].start()
-
-    def own_tap(q):
-        both = first = None
-        for p in range(3):
-            v = xo[:, p : p + rows].reshape(frames * rows * width, chans)
-            a = mm(v, w1[2, p, q])
-            b = mm(v[: rows * width], w1[1, p, q])
-            both = a if both is None else both + a
-            first = b if first is None else first + b
-        inside = slice(PAD, PAD + width)
-        acc[q, 0, :, inside, :] = both[: rows * width].reshape(rows, width, chans)
-        acc[q, 1, :, inside, :] = (both[rows * width :] + first).reshape(rows, width, chans)
-
+    load_w1_prev.wait()
     for c in range(chunks):
         forward(c)
-        if c < 3:
-            own_tap(c)
 
     def shifted_sum(ref, c0, c1):
         return sum(ref[q, ..., PAD - 1 + q + c0 : PAD - 1 + q + c1, :] for q in range(3))
@@ -179,32 +237,35 @@
     bias1 = b1_ref[...].reshape(1, 1, chans)
     bias2 = b2_ref[...].reshape(1, 1, chans)
 
-    def first_conv(c):
-        @pl.when(has_prev)
-        def _():
-            middle[c].wait_recv()
-
-        @pl.when(has_prev & has_dn)
-        def _():
-            fwd[c][0].wait_recv()
-
-        @pl.when(has_prev & has_up)
-        def _():
-            fwd[c][1].wait_recv()
-
+    def first_conv(c, unit0, unit1):
         c0, c1 = xb[c], xb[c + 1]
         size = rows * (c1 - c0)
-        for q in range(3):
-            both = second = None
-            for p in range(3):
-                v = xh[:, p : p + rows, c0:c1].reshape(frames * size, chans)
-                a = mm(v, w1[0, p, q])
-                b = mm(v[size:], w1[1, p, q])
-                both = a if both is None else both + a
-                second = b if second is None else second + b
-            inside = slice(PAD + c0, PAD + c1)
-            acc[q, 0, :, inside, :] += (both[:size] + second).reshape(rows, c1 - c0, chans)
-            acc[q, 1, :, inside, :] += both[size:].reshape(rows, c1 - c0, chans)
+
+        def left(f, p):
+            return lambda: xh[f, p : p + rows, c0:c1].reshape(size, chans)
+
+        def pair(accs, q, p):
+            return (lambda: w1[0, p, q]), [(accs[0], left(0, p)), (accs[1], left(1, p))]
+
+        def single(accs, q, p):
+            return (lambda: w1[1, p, q]), [(accs[0], left(1, p))]
+
+        @pl.when(has_prev & has_dn)
+        def _():
+            fwd[c][0].wait_recv()
+
+        @pl.when(has_prev & has_up)
+        def _():
+            fwd[c][1].wait_recv()
+
+        @pl.when(has_prev)
+        def _():
+            middle[c].wait_recv()
+            matmuls(first_jobs(unit0, unit1, pair, single))
+            store_taps(
+                unit0, unit1, lambda v: v.reshape(rows, c1 - c0, chans), slice(None), slice(PAD + c0, PAD + c1), True
+            )
+
         h0, h1 = hb[c], hb[c + 1]
         y = [shifted_sum(acc.at[:, f], h0, h1) + bias1 for f in range(2)]
         y = [(v / (1.0 + jnp.exp(-v))).astype(BF16) for v in y]
@@ -219,7 +280,7 @@
         def _():
             hid[c][1].start()
 
-    def second_conv(c):
+    def second_conv(c, unit0, unit1):
         @pl.when(has_dn)
         def _():
             hid[c][0].wait_recv()
@@ -230,18 +291,22 @@
 
         h0, h1 = hb[c], hb[c + 1]
         size = rows * (h1 - h0)
-        for q in range(3):
-            one = two = mix = None
-            for p in range(3):
-                v = hs[0, p : p + rows, h0:h1].reshape(size, chans)
-                u = hs[1, p : p + rows, h0:h1].reshape(size, chans)
-                a, b, d = mm(v, w2[1, p, q]), mm(u, w2[2, p, q]), mm(u, w01[p, q])
-                one = a if one is None else one + a
-                two = b if two is None else two + b
-                mix = d if mix is None else mix + d
-            inside = slice(PAD + h0, PAD + h1)
-            oq[q, :, inside, :] = (one + two).reshape(rows, h1 - h0, chans)
-            nq[q, :, inside, :] = (mix - one).reshape(rows, h1 - h0, chans)
+
+        def job(accs, kind, q, p):
+            weight = ((lambda: w2[1, p, q]), (lambda: w2[2, p, q]), (lambda: w01[p, q]))[kind]
+            return weight, [(accs, lambda: hs[min(kind, 1), p : p + rows, h0:h1].reshape(size, chans))]
+
+        jobs = []
+        for accs, q, extra in ((unit0, 0, ((0, 0), (0, 1), (0, 2), (1, 0))), (unit1, 2, ((2, 0), (2, 1), (2, 2), (1, 1), (1, 2)))):
+            first = [job(accs[kind], kind, q, p) for kind in range(3) for p in range(3)]
+            jobs.append(first + [job(accs[4 if kind == 1 else 3], kind, 1, p) for kind, p in extra])
+        matmuls(jobs)
+        pops = [[pltpu.matmul_pop(a).reshape(rows, h1 - h0, chans) for a in unit] for unit in (unit0, unit1)]
+        (one0, two0, mix0, one1, part0), (one2, two2, mix2, mix1, part1) = pops
+        inside = slice(PAD + h0, PAD + h1)
+        for q, one, two, mix in ((0, one0, two0, mix0), (1, one1, part0 + part1, mix1), (2, one2, two2, mix2)):
+            oq[q, :, inside, :] = one + two
+            nq[q, :, inside, :] = mix - one
         p0, p1 = pb[c], pb[c + 1]
         ns[:, p0:p1] = shifted_sum(nq, p0, p1).astype(BF16)
 
@@ -252,23 +317,25 @@
         own = xo[0, 1 : rows + 1, p0:p1].astype(F32) + xo[1, 1 : rows + 1, p0:p1].astype(F32)
         ob[:, p0:p1] = 0.5 * (shifted_sum(oq, p0, p1) + own) + bias2
 
-    first_conv(0)
+    def first(c):
+        accumulators(functools.partial(first_conv, c), rows * (xb[c + 1] - xb[c]), 4)
+
+    def second(c):
+        accumulators(functools.partial(second_conv, c), rows * (hb[c + 1] - hb[c]), 5)
+
+    first(0)
     for c in range(1, chunks):
-        first_conv(c)
-        second_conv(c - 1)
-    second_conv(chunks - 1)
-
-    stores = []
+        first(c)
+        second(c - 1)
+    second(chunks - 1)
+
     for c in range(chunks):
         @pl.when(has_prev)
         def _():
             part[c].wait_recv()
 
         p0, p1 = pb[c], pb[c + 1]
-        outv[:, p0:p1] = (ob[:, p0:p1] + 0.5 * nr[:, p0:p1].astype(F32)).astype(BF16)
-        store = local(outv.at[:, p0:p1], out_hbm.at[0, :, p0:p1], st.at[c])
-        store.start()
-        stores.append(store)
+        out[0, :, p0:p1] = (ob[:, p0:p1] + 0.5 * nr[:, p0:p1].astype(F32)).astype(BF16)
 
     @pl.when(has_next)
     def _():
@@ -297,9 +364,6 @@
     def _():
         for c in range(chunks):
             fwd[c][1].wait_send()
-
-    for store in stores:
-        store.wait()
 
 
 def shards(x, w1, b1, w2, b2):
@@ -314,14 +378,14 @@
         kernel,
         out_shape=jax.ShapeDtypeStruct((1, rows, width, chans), BF16),
         in_specs=[hbm, hbm, vmem, hbm, vmem],
-        out_specs=hbm,
+        out_specs=vmem,
         scratch_shapes=[
             extended, extended,
             pltpu.VMEM(w1.shape, BF16), pltpu.VMEM(w2.shape, BF16), pltpu.VMEM(w2.shape[1:], BF16),
             pltpu.VMEM((3, frames, rows, width + 2 * PAD, chans), F32),
             extended, taps, taps, pltpu.VMEM((rows, width, chans), F32),
-            flat, flat, flat,
-            dma((3,)), dma((chunks,)),
+            flat, flat,
+            dma((4,)), pltpu.SemaphoreType.REGULAR((2,)),
             dma((3 * chunks,)), dma((3 * chunks,)),
             dma((2,)), dma((2,)),
             dma((2 * chunks,)), dma((2 * chunks,)),

time: 45.7 us -> 41.1 us (0.90)
  Pallas kernels: 43.9 us -> 38.9 us
    pallas_call x1, Pallas kernels: 43.9 us -> 38.9 us  [shards(): pl.pallas_call(kernel, out_shape=jax.ShapeDtypeStruct((1, rows, width, ch...]
where the time goes in v2:
time: 41.1 us; the launch traced here: 40.6 us
  Pallas kernels  38.9 us (95%)
  local copies, waits for them, and re-layouts  1.67 us (4%)
    pallas_call x1, Pallas kernels, shards(): pl.pallas_call(kernel, out_shape=jax.ShapeDtypeStruct((1, rows, width, ch...  38.9 us
    unnamed x1, local copies, waits for them, and re-layouts  1.67 us

profile of v2, /device:TPU:516, one launch (start us, length us, event | category | flops | bytes accessed | tf_op | source)
XLA Modules:
  0.0 40.6 jit_solution(15746517644644842059)
XLA Ops:
  0.0 38.9 %shard_map.55 = bf16[1,4,128,256]{3,2,1,0:T(8,128)(2,1)} custom-call(bf16[2,4,128,256]{3,2,1,0:T(8,128)(2,1)} %x_hbm.1, bf16[3,3,3,256,256]{4,3,2,1,0:T(8,128)(2,1)} %w1_hbm.1, f32[1,256]{1,0:T(1,128)} %bitcast.2, bf16[3,3,3,256,256]{4,3,2,1,0:T(8,128)(2,1)} %w2_hbm.1, f32[1,256]{1,0:T(1,128)} %bitcast.3), custom_call_target="tpu_custom_call" | custom-call | tf_op jit(solution)/shard_map/pallas_call | solution.py:377
  38.9 1.7 %copy.7 = bf16[1,4,128,256]{3,2,1,0:T(8,128)(2,1)} copy(bf16[1,4,128,256]{3,2,1,0:T(8,128)(2,1)} %shard_map.55) | data formatting | bytes 524288

commit v3 on v2

--- a/solution.py
+++ b/solution.py
@@ -9,6 +9,7 @@
 
 MESH = pl.DeviceIdType.MESH
 PAD = 8
+ORDER = ((0, 0), (0, 1), (0, 2), (0, 3), (1, 0), (1, 1), (1, 2), (1, 3))
 F32 = jnp.float32
 BF16 = jnp.bfloat16
 
@@ -99,13 +100,22 @@
             xh[:, row] = zero
             hs[:, row] = zero
 
+    peers = sum(cond.astype(jnp.int32) for cond in (has_next, has_up & even, has_dn & even))
+
+    @pl.when(peers > 0)
+    def _():
+        pl.semaphore_wait(barrier, peers)
+
+    @pl.when(has_up & even)
+    def _():
+        pl.semaphore_signal(ready.at[0], inc=1, device_id=up, device_id_type=MESH)
+
+    @pl.when(has_dn & even)
+    def _():
+        pl.semaphore_signal(ready.at[1], inc=1, device_id=dn, device_id_type=MESH)
+
     accumulators(lambda unit0, unit1: [pltpu.matmul_pop(a) for a in (*unit0, *unit1)] and None, 1024, 1)
     load_x.wait()
-    peers = sum(cond.astype(jnp.int32) for cond in (has_next, has_up & even, has_dn & even))
-
-    @pl.when(peers > 0)
-    def _():
-        pl.semaphore_wait(barrier, peers)
 
     def rowcopy(buf, c0, c1, s, r, k, down):
         if down:
@@ -149,12 +159,10 @@
 
     @pl.when(has_up & even)
     def _():
-        pl.semaphore_signal(ready.at[0], inc=1, device_id=up, device_id_type=MESH)
         own_up.start()
 
     @pl.when(has_dn & even)
     def _():
-        pl.semaphore_signal(ready.at[1], inc=1, device_id=dn, device_id_type=MESH)
         own_dn.start()
 
     @pl.when(has_dn & odd)
@@ -226,7 +234,7 @@
     for r0 in (0, 2):
         accumulators(functools.partial(own_half, r0), 2 * width, 4)
     load_w2.wait()
-    w01[...] = (w2[0].astype(F32) + w2[1].astype(F32)).astype(BF16)
+    w01[...] = w2[0] + w2[1]
     load_w1_prev.wait()
     for c in range(chunks):
         forward(c)
@@ -267,8 +275,8 @@
             )
 
         h0, h1 = hb[c], hb[c + 1]
-        y = [shifted_sum(acc.at[:, f], h0, h1) + bias1 for f in range(2)]
-        y = [(v / (1.0 + jnp.exp(-v))).astype(BF16) for v in y]
+        y = [0.5 * (shifted_sum(acc.at[:, f], h0, h1) + bias1) for f in range(2)]
+        y = [(v + v * jnp.tanh(v)).astype(BF16) for v in y]
         hs[0, 1 : rows + 1, h0:h1] = y[0]
         hs[1, 1 : rows + 1, h0:h1] = (y[0].astype(F32) + y[1].astype(F32)).astype(BF16)
 
@@ -323,11 +331,8 @@
     def second(c):
         accumulators(functools.partial(second_conv, c), rows * (hb[c + 1] - hb[c]), 5)
 
-    first(0)
-    for c in range(1, chunks):
-        first(c)
-        second(c - 1)
-    second(chunks - 1)
+    for stage, c in ORDER:
+        (first, second)[stage](c)
 
     for c in range(chunks):
         @pl.when(has_prev)
@@ -376,7 +381,7 @@
     flat = pltpu.VMEM((rows, width, chans), BF16)
     return pl.pallas_call(
         kernel,
-        out_shape=jax.ShapeDtypeStruct((1, rows, width, chans), BF16),
+        out_shape=pltpu.VMEM((1, rows, width, chans), BF16),
         in_specs=[hbm, hbm, vmem, hbm, vmem],
         out_specs=vmem,
         scratch_shapes=[
@@ -393,7 +398,7 @@
             dma((chunks,)), dma((chunks,)),
         ],
         compiler_params=pltpu.CompilerParams(
-            collective_id=0, has_side_effects=True, vmem_limit_bytes=67043328
+            collective_id=0, has_side_effects=True, vmem_limit_bytes=67043328 - 600000
         ),
     )(x, w1, b1.reshape(1, chans), w2, b2.reshape(1, chans))
 

time: 41.1 us -> 38.8 us (0.944)
  Pallas kernels: 38.9 us -> 37.9 us
  local copies, waits for them, and re-layouts: 1.67 us -> 0.71 us
    unnamed x1, local copies, waits for them, and re-layouts: 1.67 us -> 0.71 us
    pallas_call x1, Pallas kernels: 38.9 us -> 37.9 us  [shards(): pl.pallas_call(kernel, out_shape=pltpu.VMEM((1, rows, width, chans), BF16...]
where the time goes in v3:
time: 38.8 us; the launch traced here: 38.7 us
  Pallas kernels  37.9 us (98%)
  local copies, waits for them, and re-layouts  0.71 us (2%)
    pallas_call x1, Pallas kernels, shards(): pl.pallas_call(kernel, out_shape=pltpu.VMEM((1, rows, width, chans), BF16...  37.9 us

profile of v3, /device:TPU:516, one launch (start us, length us, event | category | flops | bytes accessed | tf_op | source)
XLA Modules:
  0.0 38.7 jit_solution(15796115159419637004)
XLA Ops:
  0.0 37.9 %shard_map.55 = bf16[1,4,128,256]{3,2,1,0:T(8,128)(2,1)S(1)} custom-call(bf16[2,4,128,256]{3,2,1,0:T(8,128)(2,1)} %x_hbm.1, bf16[3,3,3,256,256]{4,3,2,1,0:T(8,128)(2,1)} %w1_hbm.1, f32[1,256]{1,0:T(1,128)} %bitcast.2, bf16[3,3,3,256,256]{4,3,2,1,0:T(8,128)(2,1)} %w2_hbm.1, f32[1,256]{1,0:T(1,128)} %bitcast.3), custom_call_target="tpu_custom_call" | custom-call | tf_op jit(solution)/shard_map/pallas_call | solution.py:382
  38.0 0.7 %copy.7 = bf16[1,4,128,256]{3,2,1,0:T(8,128)(2,1)} copy(bf16[1,4,128,256]{3,2,1,0:T(8,128)(2,1)S(1)} %shard_map.55) | data formatting | bytes 524288

commit v4 on v3

--- a/solution.py
+++ b/solution.py
@@ -9,7 +9,7 @@
 
 MESH = pl.DeviceIdType.MESH
 PAD = 8
-ORDER = ((0, 0), (0, 1), (0, 2), (0, 3), (1, 0), (1, 1), (1, 2), (1, 3))
+ORDER = ((0, 0), (0, 1), (0, 2), (0, 3), (1, 0), (1, 1), (1, 2), (1, 3), (2, 0), (2, 1), (2, 2), (2, 3))
 F32 = jnp.float32
 BF16 = jnp.bfloat16
 
@@ -42,8 +42,8 @@
 
 
 def kernel(
-    x_hbm, w1_hbm, b1_ref, w2_hbm, b2_ref, out,
-    xo, xh, w1, w2, w01, acc, hs, oq, nq, ob, ns, nr,
+    x_hbm, w1_hbm, b1_hbm, w2_hbm, b2_hbm, out,
+    xo, xh, w1, w2, w01, b1_ref, b2_ref, acc, hs, oq, nq, ob, ns, nr,
     ld, ready, xs_s, xs_r, ro_s, ro_r, fw_s, fw_r, he_s, he_r, n_s, n_r,
 ):
     frames, rows, width, chans = x_hbm.shape
@@ -69,10 +69,9 @@
     load_w1_own = local(w1_hbm.at[1:3], w1.at[1:3], ld.at[1])
     load_w1_prev = local(w1_hbm.at[0], w1.at[0], ld.at[2])
     load_w2 = local(w2_hbm, w2, ld.at[3])
+    load_b1 = local(b1_hbm, b1_ref, ld.at[4])
+    load_b2 = local(b2_hbm, b2_ref, ld.at[5])
     load_x.start()
-    load_w1_own.start()
-    load_w1_prev.start()
-    load_w2.start()
 
     barrier = pltpu.get_barrier_semaphore()
     odd = lax.rem(j, 2) == 1
@@ -82,24 +81,6 @@
         def _(dev=dev):
             pl.semaphore_signal(barrier, inc=1, device_id=dev, device_id_type=MESH)
 
-    for buf in (oq, nq):
-        for q, at in ((0, 0), (2, PAD + width)):
-            buf[q, :, at : at + PAD, :] = jnp.zeros((rows, PAD, chans), F32)
-    for q, at in ((0, 0), (2, PAD + width)):
-        acc[q, :, :, at : at + PAD, :] = jnp.zeros((frames, rows, PAD, chans), F32)
-
-    @pl.when(jnp.logical_not(has_prev))
-    def _():
-        nr[...] = jnp.zeros(nr.shape, BF16)
-
-    for cond, row in ((has_up, 0), (has_dn, last + 1)):
-        @pl.when(jnp.logical_not(cond))
-        def _(row=row):
-            zero = jnp.zeros((frames, width, chans), BF16)
-            xo[:, row] = zero
-            xh[:, row] = zero
-            hs[:, row] = zero
-
     peers = sum(cond.astype(jnp.int32) for cond in (has_next, has_up & even, has_dn & even))
 
     @pl.when(peers > 0)
@@ -114,7 +95,6 @@
     def _():
         pl.semaphore_signal(ready.at[1], inc=1, device_id=dn, device_id_type=MESH)
 
-    accumulators(lambda unit0, unit1: [pltpu.matmul_pop(a) for a in (*unit0, *unit1)] and None, 1024, 1)
     load_x.wait()
 
     def rowcopy(buf, c0, c1, s, r, k, down):
@@ -165,6 +145,31 @@
     def _():
         own_dn.start()
 
+    load_w1_own.start()
+    load_w1_prev.start()
+    load_w2.start()
+    load_b1.start()
+    load_b2.start()
+    accumulators(lambda unit0, unit1: [pltpu.matmul_pop(a) for a in (*unit0, *unit1)] and None, 1024, 1)
+
+    for buf in (oq, nq):
+        for q, at in ((0, 0), (2, PAD + width)):
+            buf[q, :, at : at + PAD, :] = jnp.zeros((rows, PAD, chans), F32)
+    for q, at in ((0, 0), (2, PAD + width)):
+        acc[q, :, :, at : at + PAD, :] = jnp.zeros((frames, rows, PAD, chans), F32)
+
+    @pl.when(jnp.logical_not(has_prev))
+    def _():
+        nr[...] = jnp.zeros(nr.shape, BF16)
+
+    for cond, row in ((has_up, 0), (has_dn, last + 1)):
+        @pl.when(jnp.logical_not(cond))
+        def _(row=row):
+            zero = jnp.zeros((frames, width, chans), BF16)
+            xo[:, row] = zero
+            xh[:, row] = zero
+            hs[:, row] = zero
+
     @pl.when(has_dn & odd)
     def _():
         pl.semaphore_wait(ready.at[0], 1)
@@ -236,9 +241,8 @@
     load_w2.wait()
     w01[...] = w2[0] + w2[1]
     load_w1_prev.wait()
-    for c in range(chunks):
-        forward(c)
-
+    load_b1.wait()
+    load_b2.wait()
     def shifted_sum(ref, c0, c1):
         return sum(ref[q, ..., PAD - 1 + q + c0 : PAD - 1 + q + c1, :] for q in range(3))
 
@@ -332,7 +336,7 @@
         accumulators(functools.partial(second_conv, c), rows * (hb[c + 1] - hb[c]), 5)
 
     for stage, c in ORDER:
-        (first, second)[stage](c)
+        (forward, first, second)[stage](c)
 
     for c in range(chunks):
         @pl.when(has_prev)
@@ -382,15 +386,16 @@
     return pl.pallas_call(
         kernel,
         out_shape=pltpu.VMEM((1, rows, width, chans), BF16),
-        in_specs=[hbm, hbm, vmem, hbm, vmem],
+        in_specs=[hbm] * 5,
         out_specs=vmem,
         scratch_shapes=[
             extended, extended,
             pltpu.VMEM(w1.shape, BF16), pltpu.VMEM(w2.shape, BF16), pltpu.VMEM(w2.shape[1:], BF16),
+            pltpu.VMEM((1, chans), F32), pltpu.VMEM((1, chans), F32),
             pltpu.VMEM((3, frames, rows, width + 2 * PAD, chans), F32),
             extended, taps, taps, pltpu.VMEM((rows, width, chans), F32),
             flat, flat,
-            dma((4,)), pltpu.SemaphoreType.REGULAR((2,)),
+            dma((6,)), pltpu.SemaphoreType.REGULAR((2,)),
             dma((3 * chunks,)), dma((3 * chunks,)),
             dma((2,)), dma((2,)),
             dma((2 * chunks,)), dma((2 * chunks,)),

time: 38.8 us -> 38 us (0.979)
  Pallas kernels: 37.9 us -> 37.2 us
    pallas_call x1, Pallas kernels: 37.9 us -> 37.2 us  [shards(): pl.pallas_call(kernel, out_shape=pltpu.VMEM((1, rows, width, chans), BF16...]
where the time goes in v4:
time: 38 us; the launch traced here: 37.9 us
  Pallas kernels  37.2 us (98%)
  local copies, waits for them, and re-layouts  0.71 us (2%)
    pallas_call x1, Pallas kernels, shards(): pl.pallas_call(kernel, out_shape=pltpu.VMEM((1, rows, width, chans), BF16...  37.2 us

profile of v4, /device:TPU:516, one launch (start us, length us, event | category | flops | bytes accessed | tf_op | source)
XLA Modules:
  0.0 37.9 jit_solution(16052320369174416919)
XLA Ops:
  0.0 37.2 %shard_map.55 = bf16[1,4,128,256]{3,2,1,0:T(8,128)(2,1)S(1)} custom-call(bf16[2,4,128,256]{3,2,1,0:T(8,128)(2,1)} %x_hbm.1, bf16[3,3,3,256,256]{4,3,2,1,0:T(8,128)(2,1)} %w1_hbm.1, f32[1,256]{1,0:T(1,128)} %bitcast.2, bf16[3,3,3,256,256]{4,3,2,1,0:T(8,128)(2,1)} %w2_hbm.1, f32[1,256]{1,0:T(1,128)} %bitcast.3), custom_call_target="tpu_custom_call" | custom-call | tf_op jit(solution)/shard_map/pallas_call | solution.py:386
  37.2 0.7 %copy.7 = bf16[1,4,128,256]{3,2,1,0:T(8,128)(2,1)} copy(bf16[1,4,128,256]{3,2,1,0:T(8,128)(2,1)S(1)} %shard_map.55) | data formatting | bytes 524288

commit v5 on v4

--- a/solution.py
+++ b/solution.py
@@ -9,7 +9,7 @@
 
 MESH = pl.DeviceIdType.MESH
 PAD = 8
-ORDER = ((0, 0), (0, 1), (0, 2), (0, 3), (1, 0), (1, 1), (1, 2), (1, 3), (2, 0), (2, 1), (2, 2), (2, 3))
+ORDER = ((0, 0), (0, 1), (0, 2), (1, 0), (1, 1), (1, 2), (2, 0), (2, 1), (2, 2), (2, 3))
 F32 = jnp.float32
 BF16 = jnp.bfloat16
 
@@ -35,10 +35,11 @@
 
 def bounds(width):
     step = width // 4
-    xs = [0, step + 16, 2 * step + 16, 3 * step + 16, width]
-    hs = [0, step, 2 * step, 3 * step, width]
-    os = [0, step - 16, 2 * step - 16, 3 * step - 16, width]
-    return xs, hs, os
+    xs = [0, step + 16, 2 * step + 16, width]
+    hs = [0, step, 2 * step, width]
+    ss = [0, step, 2 * step, 3 * step, width]
+    ps = [0, step - 16, 2 * step - 16, 3 * step - 16, width]
+    return xs, hs, ss, ps
 
 
 def kernel(
@@ -47,8 +48,8 @@
     ld, ready, xs_s, xs_r, ro_s, ro_r, fw_s, fw_r, he_s, he_r, n_s, n_r,
 ):
     frames, rows, width, chans = x_hbm.shape
-    xb, hb, pb = bounds(width)
-    chunks = len(xb) - 1
+    xb, hb, sb, pb = bounds(width)
+    chunks, pieces = len(xb) - 1, len(pb) - 1
     i, j = lax.axis_index("tm"), lax.axis_index("tile")
     ni, nj = lax.axis_size("tm"), lax.axis_size("tile")
     has_prev, has_next = i > 0, i < ni - 1
@@ -65,13 +66,17 @@
             src_ref=src, dst_ref=dst, send_sem=ssem, recv_sem=rsem, device_id=dev, device_id_type=MESH
         )
 
-    load_x = local(x_hbm, xo.at[:, 1 : rows + 1], ld.at[0])
+    load_x = [
+        local(x_hbm.at[:, a:b], xo.at[:, a + 1 : b + 1], ld.at[k])
+        for k, a, b in ((0, 0, 1), (6, rows - 1, rows), (7, 1, rows - 1))
+    ]
     load_w1_own = local(w1_hbm.at[1:3], w1.at[1:3], ld.at[1])
     load_w1_prev = local(w1_hbm.at[0], w1.at[0], ld.at[2])
     load_w2 = local(w2_hbm, w2, ld.at[3])
     load_b1 = local(b1_hbm, b1_ref, ld.at[4])
     load_b2 = local(b2_hbm, b2_ref, ld.at[5])
-    load_x.start()
+    for load in load_x:
+        load.start()
 
     barrier = pltpu.get_barrier_semaphore()
     odd = lax.rem(j, 2) == 1
@@ -95,7 +100,8 @@
     def _():
         pl.semaphore_signal(ready.at[1], inc=1, device_id=dn, device_id_type=MESH)
 
-    load_x.wait()
+    for load in load_x[:2]:
+        load.wait()
 
     def rowcopy(buf, c0, c1, s, r, k, down):
         if down:
@@ -126,7 +132,7 @@
     ]
     part = [
         remote(ns.at[:, pb[c] : pb[c + 1]], nr.at[:, pb[c] : pb[c + 1]], n_s.at[c], n_r.at[c], nxt)
-        for c in range(chunks)
+        for c in range(pieces)
     ]
 
     @pl.when(has_next)
@@ -134,6 +140,11 @@
         for pair in edges:
             for copy in pair:
                 copy.start()
+
+    load_x[2].wait()
+
+    @pl.when(has_next)
+    def _():
         for copy in middle:
             copy.start()
 
@@ -293,15 +304,16 @@
             hid[c][1].start()
 
     def second_conv(c, unit0, unit1):
-        @pl.when(has_dn)
-        def _():
-            hid[c][0].wait_recv()
-
-        @pl.when(has_up)
-        def _():
-            hid[c][1].wait_recv()
-
-        h0, h1 = hb[c], hb[c + 1]
+        if c < chunks:
+            @pl.when(has_dn)
+            def _():
+                hid[c][0].wait_recv()
+
+            @pl.when(has_up)
+            def _():
+                hid[c][1].wait_recv()
+
+        h0, h1 = sb[c], sb[c + 1]
         size = rows * (h1 - h0)
 
         def job(accs, kind, q, p):
@@ -333,12 +345,12 @@
         accumulators(functools.partial(first_conv, c), rows * (xb[c + 1] - xb[c]), 4)
 
     def second(c):
-        accumulators(functools.partial(second_conv, c), rows * (hb[c + 1] - hb[c]), 5)
+        accumulators(functools.partial(second_conv, c), rows * (sb[c + 1] - sb[c]), 5)
 
     for stage, c in ORDER:
         (forward, first, second)[stage](c)
 
-    for c in range(chunks):
+    for c in range(pieces):
         @pl.when(has_prev)
         def _():
             part[c].wait_recv()
@@ -349,8 +361,10 @@
     @pl.when(has_next)
     def _():
         for c in range(chunks):
-            for copy in (*edges[c], middle[c], part[c]):
+            for copy in (*edges[c], middle[c]):
                 copy.wait_send()
+        for copy in part:
+            copy.wait_send()
 
     @pl.when(has_up)
     def _():
@@ -377,7 +391,7 @@
 
 def shards(x, w1, b1, w2, b2):
     frames, rows, width, chans = x.shape
-    chunks = len(bounds(width)[0]) - 1
+    chunks, pieces = (len(bounds(width)[k]) - 1 for k in (0, 3))
     dma = pltpu.SemaphoreType.DMA
     hbm, vmem = pl.BlockSpec(memory_space=pltpu.HBM), pl.BlockSpec(memory_space=pltpu.VMEM)
     extended = pltpu.VMEM((frames, rows + 2, width, chans), BF16)
@@ -395,12 +409,12 @@
             pltpu.VMEM((3, frames, rows, width + 2 * PAD, chans), F32),
             extended, taps, taps, pltpu.VMEM((rows, width, chans), F32),
             flat, flat,
-            dma((6,)), pltpu.SemaphoreType.REGULAR((2,)),
+            dma((8,)), pltpu.SemaphoreType.REGULAR((2,)),
             dma((3 * chunks,)), dma((3 * chunks,)),
             dma((2,)), dma((2,)),
             dma((2 * chunks,)), dma((2 * chunks,)),
             dma((2 * chunks,)), dma((2 * chunks,)),
-            dma((chunks,)), dma((chunks,)),
+            dma((pieces,)), dma((pieces,)),
         ],
         compiler_params=pltpu.CompilerParams(
             collective_id=0, has_side_effects=True, vmem_limit_bytes=67043328 - 600000

time: 38 us -> 37.9 us (level)
  no operation moved by 1% of the time
where the time goes in v5:
time: 37.9 us; the launch traced here: 37.8 us
  Pallas kernels  37.1 us (98%)
  local copies, waits for them, and re-layouts  0.71 us (2%)
    pallas_call x1, Pallas kernels, shards(): pl.pallas_call(kernel, out_shape=pltpu.VMEM((1, rows, width, chans), BF16...  37.1 us

profile of v5, /device:TPU:516, one launch (start us, length us, event | category | flops | bytes accessed | tf_op | source)
XLA Modules:
  0.0 37.8 jit_solution(6131173820586818242)
XLA Ops:
  0.0 37.1 %shard_map.55 = bf16[1,4,128,256]{3,2,1,0:T(8,128)(2,1)S(1)} custom-call(bf16[2,4,128,256]{3,2,1,0:T(8,128)(2,1)} %x_hbm.1, bf16[3,3,3,256,256]{4,3,2,1,0:T(8,128)(2,1)} %w1_hbm.1, f32[1,256]{1,0:T(1,128)} %bitcast.2, bf16[3,3,3,256,256]{4,3,2,1,0:T(8,128)(2,1)} %w2_hbm.1, f32[1,256]{1,0:T(1,128)} %bitcast.3), custom_call_target="tpu_custom_call" | custom-call | tf_op jit(solution)/shard_map/pallas_call | solution.py:400
  37.1 0.7 %copy.7 = bf16[1,4,128,256]{3,2,1,0:T(8,128)(2,1)} copy(bf16[1,4,128,256]{3,2,1,0:T(8,128)(2,1)S(1)} %shard_map.55) | data formatting | bytes 524288
